TPU v7x, 32 devices: a whole 2x2x4 slice. The times are simulated.
32 devices in a mesh: lat: 4 (over y, x), lon: 8 (over z, core).
Axes of the slice: x: 2, y: 2, z: 4, core: 2. Of those that a mesh axis runs over, the one named last changes fastest.
Arguments:
- adjoint_in: bfloat16 [8, 100, 8, 1024], P(None, None, 'lat', 'lon'), may hold values from -6 to 6
- state: bfloat16 [2, 8, 100, 8, 1024], P(None, None, None, 'lat', 'lon'), may hold values from 0.29882812 to 1
- inverses: bfloat16 [3, 8, 100, 100], replicated
- courant_lon: float32 [8, 1024], P('lat', 'lon'), may hold values from 0.1 to 0.4
- courant_lat: float32 [8, 1024], P('lat', 'lon'), may hold values from 0.1 to 0.4
- emission: float32 [100, 8, 1024], P(None, 'lat', 'lon'), may hold values from 0.02 to 0.2
- region_id: int32 [8, 1024], P('lat', 'lon'), may hold values from 0 to 31, as said below
- stiffness: int32 [8, 8, 1024], P(None, 'lat', 'lon'), may hold values from 1 to 3
Outputs:
- adjoint_out: bfloat16 [8, 100, 8, 1024], P(None, None, 'lat', 'lon')
- emission_grad: float32 [32, 100], P(('lat', 'lon'))
Inputs may be any that keep to these rules, and one draw needn't show every extreme that they name: `region_id`: constant on aligned tiles of 2 x 2 columns.
All inputs are finite; a program needn't handle non-finite values.
Results may differ from a plain program's by a relative error of at most 0.0048.
Values sent between devices are 32-bit elements; how exact they have to be, the bound alone decides.
A program may use at most 64 MiB of HBM per device.

v0:
```python
import jax
import jax.numpy as jnp
from jax import lax
from jax.sharding import PartitionSpec as P

STEPS = 3
NWIN = 2
ADV = 2
REG_DEV = 1


def shifted(block, axis, distance):
    devices = range(lax.axis_size(axis))
    route = [((i - distance) % len(devices), i) for i in devices]
    return lax.ppermute(block, axis, route)


def from_behind(block, axis, distance):
    devices = range(lax.axis_size(axis))
    route = [(i - distance, i) for i in devices if i - distance in devices]
    return lax.ppermute(block, axis, route)


def advect(lam, clon, clat, east, south):
    right = jnp.concatenate([lam[:, :, :, 1:], east], axis=3)
    down = jnp.concatenate([lam[:, :, 1:, :], south], axis=2)
    return (1.0 - clon - clat) * lam + clat * down + clon * right


def transport_each(lam, courant_lon, courant_lat):
    for k in range(ADV):
        east = shifted(lam[:, :, :, :1], "lon", -1)
        south = from_behind(lam[:, :, :1, :], "lat", -1)
        lam = advect(lam, courant_lon, courant_lat, east, south)
    return lam


def transposed(mats, right_side):
    return lax.dot_general(
        mats, right_side, (((1,), (1,)), ((0,), (0,))), preferred_element_type=jnp.float32
    )


def chemistry(lam, factor, inverses, stiffness):
    levels, spec, rows, cols = lam.shape
    flat = lam.reshape(levels, spec, rows * cols)
    yfac = factor.reshape(levels, spec, rows * cols)
    live = stiffness.reshape(levels, 1, rows * cols)
    for s in reversed(range(STEPS)):
        mats = inverses[s]

        def advance(values, mats=mats, s=s):
            first = transposed(mats, values.astype(jnp.bfloat16))
            second = transposed(mats, (first * yfac).astype(jnp.bfloat16))
            third = transposed(mats, (second * yfac).astype(jnp.bfloat16))
            cand = 0.4 * values + 0.3 * first + 0.2 * second + 0.1 * third
            return jnp.where(live > s, cand, values)

        flat = lax.cond(jnp.any(stiffness > s), advance, lambda values: values, flat)
    return flat.reshape(levels, spec, rows, cols)


def per_device(
    adjoint_in, state, inverses, courant_lon, courant_lat, emission, region_id, stiffness
):
    lam = adjoint_in.astype(jnp.float32)
    surface = jnp.zeros(emission.shape, jnp.float32)
    for window in reversed(range(NWIN)):
        lam = transport_each(lam, courant_lon, courant_lat)
        lam = chemistry(lam, state[window], inverses, stiffness)
        surface = surface + lam[0]
    spec = emission.shape[0]
    regions = REG_DEV * lax.axis_size("lat") * lax.axis_size("lon")
    contrib = (surface * emission).reshape(spec, -1)
    labels = lax.broadcasted_iota(jnp.int32, (regions, contrib.shape[1]), 0)
    onehot = (region_id.reshape(1, -1) == labels).astype(jnp.float32)
    partial_value = lax.dot_general(
        onehot,
        contrib,
        (((1,), (1,)), ((), ())),
        precision=lax.Precision.HIGHEST,
        preferred_element_type=jnp.float32,
    )
    total = lax.psum(partial_value, ("lat", "lon"))
    share = REG_DEV
    grad = lax.dynamic_slice_in_dim(total, lax.axis_index(("lat", "lon")) * share, share, 0)
    return (lam.astype(jnp.bfloat16), grad)


def solution(mesh):
    in_specs = (
        P(None, None, "lat", "lon"),
        P(None, None, None, "lat", "lon"),
        P(),
        P("lat", "lon"),
        P("lat", "lon"),
        P(None, "lat", "lon"),
        P("lat", "lon"),
        P(None, "lat", "lon"),
    )
    out_specs = (P(None, None, "lat", "lon"), P(("lat", "lon"), None))
    return jax.shard_map(
        per_device, mesh=mesh, in_specs=in_specs, out_specs=out_specs, check_vma=False
    )
```

profile of v0, /device:TPU:0, one launch (start us, length us, event | category | flops | bytes accessed | tf_op | source)
XLA Modules:
  0.0 117.9 jit_solution(164117389838447661)
XLA Ops:
  0.6 1.1 copy_convert_fusion.5
  1.7 0.8 fusion.83
  2.5 1.3 %collective-permute-start = (f32[8,100,1,128]{3,0,2,1:T(8,128)}, f32[8,100,1,128]{3,0,2,1:T(8,128)}, u32[]{:S(2)}, u32[]{:S(2)}) collective-permute-start(f32[8,100,1,128]{3,0,2,1:T(8,128)} %get-tuple-element.166), channel_id=1, source_target_pairs={{8,0},{16,8},{24,16},{9,1},{17,9},{25,17},{10,2},{18,10},{26,18},{... | collective-permute-start | bytes 1228808 | tf_op jit(solution)/shard_map/ppermute | solution.py:21
  4.2 4.5 %collective-permute-start.1 = (f32[8,100,2,1]{1,0,3,2:T(8,128)S(1)}, f32[8,100,2,1]{1,0,3,2:T(8,128)S(1)}, u32[]{:S(2)}, u32[]{:S(2)}) collective-permute-start(f32[8,100,2,1]{1,0,3,2:T(8,128)S(1)} %copy.34), channel_id=1, source_target_pairs={{1,0},{2,1},{3,2},{4,3},{5,4},{6,5},{7,6},{0,7},{9,8},{10,9},{11,1... | collective-permute-start | bytes 19208 | tf_op jit(solution)/shard_map/ppermute | solution.py:15
  9.0 1.1 collective-permute-done.1
  10.5 6.6 %collective-permute-done = f32[8,100,1,128]{3,0,2,1:T(8,128)} collective-permute-done((f32[8,100,1,128]{3,0,2,1:T(8,128)}, f32[8,100,1,128]{3,0,2,1:T(8,128)}, u32[]{:S(2)}, u32[]{:S(2)}) %collective-permute-start) | collective-permute-done | bytes 409632 | tf_op jit(solution)/shard_map/ppermute | solution.py:21
  17.1 1.3 %fusion.65 = f32[8,100,2,128]{3,0,2,1:T(8,128)S(1)} fusion(f32[8,100,1,128]{3,0,2,1:T(8,128)} %collective-permute-done, f32[8,100,1,128]{3,0,2,1:T(8,128)S(1)} %get-tuple-element.165, f32[8,100,2,1]{3,0,2,1:T(8,128)S(1)} %copy.35, f32[8,100,2,127]{3,0,2,1:T(8,128)S(1)} %slice.99, f32[2,128]{1,0:T(2,128)S(1)} %copy-done.7, f32[2,128]{1,0:T(2,128)S(1)} %copy-done.8, ...), kind=kLoop, calls=%fused_computation.86 | loop fusion | flops 1638400 | bytes 2870272 | tf_op jit(solution)/shard_map/add | solution.py:27
  18.5 0.9 fusion.82
  19.4 1.4 %collective-permute-start.2 = (f32[8,100,1,128]{3,0,2,1:T(8,128)}, f32[8,100,1,128]{3,0,2,1:T(8,128)}, u32[]{:S(2)}, u32[]{:S(2)}) collective-permute-start(f32[8,100,1,128]{3,0,2,1:T(8,128)} %get-tuple-element.164), channel_id=1, source_target_pairs={{8,0},{16,8},{24,16},{9,1},{17,9},{25,17},{10,2},{18,10},{26,18},{... | collective-permute-start | bytes 1228808 | tf_op jit(solution)/shard_map/ppermute | solution.py:21
  20.9 1.3 %fusion.79 = (bf16[1,8,100,2,128]{4,3,2,1,0:T(2,128)(2,1)}, bf16[1,8,100,2,128]{4,3,2,1,0:T(2,128)(2,1)S(1)}) fusion(bf16[2,8,100,2,128]{4,3,2,1,0:T(2,128)(2,1)S(1)} %copy-done.3), kind=kLoop, calls=%fused_computation.122 | loop fusion | bytes 1638400 | tf_op jit(solution)/shard_map/slice | solution.py:70
  22.6 2.4 %collective-permute-start.3 = (f32[8,100,2,1]{1,0,3,2:T(8,128)S(1)}, f32[8,100,2,1]{1,0,3,2:T(8,128)}, u32[]{:S(2)}, u32[]{:S(2)}) collective-permute-start(f32[8,100,2,1]{1,0,3,2:T(8,128)S(1)} %copy.36), channel_id=1, source_target_pairs={{1,0},{2,1},{3,2},{4,3},{5,4},{6,5},{7,6},{0,7},{9,8},{10,9},{11,1... | collective-permute-start | bytes 19208 | tf_op jit(solution)/shard_map/ppermute | solution.py:15
  25.1 0.7 compare_reduce_fusion
  28.8 1.1 copy.37
  30.0 3.0 %collective-permute-done.2 = f32[8,100,1,128]{3,0,2,1:T(8,128)} collective-permute-done((f32[8,100,1,128]{3,0,2,1:T(8,128)}, f32[8,100,1,128]{3,0,2,1:T(8,128)}, u32[]{:S(2)}, u32[]{:S(2)}) %collective-permute-start.2) | collective-permute-done | bytes 409632 | tf_op jit(solution)/shard_map/ppermute | solution.py:21
  33.0 1.4 %fusion.68 = f32[8,100,256]{2,0,1:T(8,128)S(1)} fusion(f32[8,100,1,128]{3,0,2,1:T(8,128)} %collective-permute-done.2, f32[8,100,1,128]{3,0,2,1:T(8,128)} %get-tuple-element.163, f32[8,100,2,1]{3,0,2,1:T(8,128)S(1)} %copy.37, f32[8,100,2,127]{3,0,2,1:T(8,128)S(1)} %slice.103, f32[8,100,2,128]{3,0,2,1:T(8,128)S(1)} %fusion.65, f32[2,128]{1,0:T(2,128)S(1)} %copy-done.7, ...), kind=kLoop, calls=%fused_computation.91 | loop fusion | flops 1433600 | bytes 3279872 | tf_op jit(solution)/shard_map/reshape | solution.py:46
  34.4 1.3 %conditional.6 = (f32[8,100,256]{2,1,0:T(8,128)S(1)}) conditional(s32[]{:T(128)} %convert_element_type.102, (f32[8,100,256]{2,0,1:T(8,128)S(1)}) %tuple.65, (s32[8,1,256]{2,0,1:T(8,128)S(1)}, f32[8,100,256]{2,0,1:T(8,128)S(1)}, bf16[8,100,100]{1,2,0:T(8,128)(2,1)S(1)}, bf16[8,100,256]{2,0,1:T(8,128)(2,1)S(1)}) %tuple.94), branch_computations={%region_3.4_spmd, %region_4.5_spmd} | conditional | flops 125749248 | bytes 7865096 | solution.py:59
  35.2 0.6 fusion.2
  35.8 1.3 %conditional.7 = (f32[8,100,256]{2,1,0:T(8,128)S(1)}) conditional(s32[]{:T(128)} %convert_element_type.101, f32[8,100,256]{2,1,0:T(8,128)S(1)} %get-tuple-element.170, (s32[8,1,256]{2,0,1:T(8,128)S(1)}, f32[8,100,256]{2,1,0:T(8,128)S(1)}, bf16[8,100,100]{1,2,0:T(8,128)(2,1)S(1)}, bf16[8,100,256]{2,0,1:T(8,128)(2,1)S(1)}) %tuple.98), branch_computations={%region_5.6_spmd, %region_6.7_spmd} | conditional | flops 125954048 | bytes 7865096 | solution.py:59
  36.4 0.8 fusion.12
  37.1 1.3 %conditional.8 = (f32[8,100,256]{2,1,0:T(8,128)S(1)}) conditional(s32[]{:T(128)} %convert_element_type.100, f32[8,100,256]{2,1,0:T(8,128)S(1)} %get-tuple-element.171, (s32[8,1,256]{2,0,1:T(8,128)S(1)}, f32[8,100,256]{2,1,0:T(8,128)S(1)}, bf16[8,100,100]{1,2,0:T(8,128)(2,1)S(1)}, bf16[8,100,256]{2,0,1:T(8,128)(2,1)S(1)}) %tuple.96), branch_computations={%region_7.8_spmd, %region_8.9_spmd} | conditional | flops 125954048 | bytes 7865096 | solution.py:59
  37.7 0.8 fusion.23
  38.7 0.8 fusion.81
  39.5 1.3 %collective-permute-start.4 = (f32[8,100,1,128]{3,0,2,1:T(8,128)}, f32[8,100,1,128]{3,0,2,1:T(8,128)}, u32[]{:S(2)}, u32[]{:S(2)}) collective-permute-start(f32[8,100,1,128]{3,0,2,1:T(8,128)} %get-tuple-element.162), channel_id=1, source_target_pairs={{8,0},{16,8},{24,16},{9,1},{17,9},{25,17},{10,2},{18,10},{26,18},{... | collective-permute-start | bytes 1228808 | tf_op jit(solution)/shard_map/ppermute | solution.py:21
  40.8 1.0 copy.49
  42.6 1.3 %collective-permute-done.5 = f32[8,100,2,1]{1,0,3,2:T(8,128)} collective-permute-done((f32[8,100,2,1]{1,0,3,2:T(8,128)}, f32[8,100,2,1]{1,0,3,2:T(8,128)}, u32[]{:S(2)}, u32[]{:S(2)}) %collective-permute-start.5) | collective-permute-done | bytes 6432 | tf_op jit(solution)/shard_map/ppermute | solution.py:15
  43.9 2.0 %copy.50 = f32[8,100,2,1]{3,0,2,1:T(8,128)} copy(f32[8,100,2,1]{1,0,3,2:T(8,128)} %collective-permute-done.5) | data formatting | bytes 12800 | tf_op jit(solution)/shard_map/ppermute | solution.py:15
  45.9 6.2 %collective-permute-done.4 = f32[8,100,1,128]{3,0,2,1:T(8,128)} collective-permute-done((f32[8,100,1,128]{3,0,2,1:T(8,128)}, f32[8,100,1,128]{3,0,2,1:T(8,128)}, u32[]{:S(2)}, u32[]{:S(2)}) %collective-permute-start.4) | collective-permute-done | bytes 409632 | tf_op jit(solution)/shard_map/ppermute | solution.py:21
  52.1 1.7 %multiply_add_fusion = f32[8,100,2,128]{3,0,2,1:T(8,128)S(1)} fusion(f32[8,100,1,128]{3,0,2,1:T(8,128)} %collective-permute-done.4, f32[8,100,1,128]{3,0,2,1:T(8,128)S(1)} %get-tuple-element.161, f32[2,128]{1,0:T(2,128)S(1)} %copy-done.7, f32[2,128]{1,0:T(2,128)S(1)} %copy-done.8, f32[2,128]{1,0:T(2,128)S(1)} %copy-done.11, f32[8,100,2,1]{3,0,2,1:T(8,128)} %copy.50, ...), kind=kLoop, calls=%fused_computation.107 | loop fusion | flops 1433600 | bytes 3279872 | tf_op jit(solution)/shard_map/add | solution.py:27
  53.8 0.9 fusion.80
  54.8 1.3 %collective-permute-start.6 = (f32[8,100,1,128]{3,0,2,1:T(8,128)}, f32[8,100,1,128]{3,0,2,1:T(8,128)}, u32[]{:S(2)}, u32[]{:S(2)}) collective-permute-start(f32[8,100,1,128]{3,0,2,1:T(8,128)} %get-tuple-element.160), channel_id=1, source_target_pairs={{8,0},{16,8},{24,16},{9,1},{17,9},{25,17},{10,2},{18,10},{26,18},{... | collective-permute-start | bytes 1228808 | tf_op jit(solution)/shard_map/ppermute | solution.py:21
  56.1 1.0 copy.51
  57.0 0.8 collective-permute-start.7
  57.8 1.1 copy.137
  58.9 1.2 %slice.111 = f32[8,100,2,127]{3,0,2,1:T(8,128)} slice(f32[8,100,2,128]{3,0,2,1:T(8,128)S(1)} %multiply_add_fusion), slice={[0:8], [0:100], [0:2], [1:128]} | slice | bytes 1625600 | tf_op jit(solution)/shard_map/slice | solution.py:25
  60.1 2.0 %copy.52 = f32[8,100,2,1]{3,0,2,1:T(8,128)} copy(f32[8,100,2,1]{1,0,3,2:T(8,128)} %collective-permute-done.7) | data formatting | bytes 12800 | tf_op jit(solution)/shard_map/ppermute | solution.py:15
  62.1 4.4 %collective-permute-done.6 = f32[8,100,1,128]{3,0,2,1:T(8,128)} collective-permute-done((f32[8,100,1,128]{3,0,2,1:T(8,128)}, f32[8,100,1,128]{3,0,2,1:T(8,128)}, u32[]{:S(2)}, u32[]{:S(2)}) %collective-permute-start.6) | collective-permute-done | bytes 409632 | tf_op jit(solution)/shard_map/ppermute | solution.py:21
  66.5 0.7 copy-done.12
  67.2 2.5 %fusion.71 = f32[8,100,256]{2,0,1:T(8,128)S(1)} fusion(f32[8,100,1,128]{3,0,2,1:T(8,128)} %collective-permute-done.6, f32[8,100,1,128]{3,0,2,1:T(8,128)} %get-tuple-element.159, f32[8,100,2,1]{3,0,2,1:T(8,128)} %copy.52, f32[8,100,2,127]{3,0,2,1:T(8,128)} %slice.111, f32[8,100,256]{2,1,0:T(8,128)S(1)} %get-tuple-element.172, ...), kind=kLoop, calls=%fused_computation.98 | loop fusion | flops 2867200 | bytes 4918272 | tf_op jit(solution)/shard_map/add | solution.py:27
  69.7 1.5 %conditional.9 = (f32[8,100,256]{2,1,0:T(8,128)S(1)}) conditional(s32[]{:T(128)} %convert_element_type.102, (f32[8,100,256]{2,0,1:T(8,128)S(1)}) %tuple.66, (s32[8,1,256]{2,0,1:T(8,128)S(1)}, f32[8,100,256]{2,0,1:T(8,128)S(1)}, bf16[8,100,100]{1,2,0:T(8,128)(2,1)S(1)}, bf16[8,100,256]{2,0,1:T(8,128)(2,1)S(1)}) %tuple.95), branch_computations={%region_9.10_spmd, %region_10.11_spmd} | conditional | flops 125749248 | bytes 7865096 | solution.py:59
  70.6 0.6 fusion.34
  71.2 1.3 %conditional.10 = (f32[8,100,256]{2,1,0:T(8,128)S(1)}) conditional(s32[]{:T(128)} %convert_element_type.101, f32[8,100,256]{2,1,0:T(8,128)S(1)} %get-tuple-element.173, (s32[8,1,256]{2,0,1:T(8,128)S(1)}, f32[8,100,256]{2,1,0:T(8,128)S(1)}, bf16[8,100,100]{1,2,0:T(8,128)(2,1)S(1)}, bf16[8,100,256]{2,0,1:T(8,128)(2,1)S(1)}) %tuple.99), branch_computations={%region_11.12_spmd, %region_12.13_spmd} | conditional | flops 125954048 | bytes 7865096 | solution.py:59
  71.8 0.8 fusion.44
  72.5 1.3 %conditional.11 = (f32[8,100,256]{2,1,0:T(8,128)S(1)}) conditional(s32[]{:T(128)} %convert_element_type.100, f32[8,100,256]{2,1,0:T(8,128)S(1)} %get-tuple-element.174, (s32[8,1,256]{2,0,1:T(8,128)S(1)}, f32[8,100,256]{2,1,0:T(8,128)S(1)}, bf16[8,100,100]{1,2,0:T(8,128)(2,1)S(1)}, bf16[8,100,256]{2,0,1:T(8,128)(2,1)S(1)}) %tuple.97), branch_computations={%region_13.14_spmd, %region_14.15_spmd} | conditional | flops 125954048 | bytes 7865096 | solution.py:59
  73.1 0.8 fusion.55
  74.2 0.8 copy-done.5
  75.2 0.7 copy-done.13
  76.0 40.3 %psum.7 = f32[32,100]{1,0:T(8,128)S(1)} all-reduce(f32[32,100]{1,0:T(8,128)S(1)} %fusion.77), channel_id=1, replica_groups=mesh['lat'=4,'lon'=8] {'lat','lon'}, use_global_device_ids=true, to_apply=%region_15.16 | all-reduce | flops 3200 | bytes 25600 | tf_op jit(solution)/shard_map/psum | solution.py:84
  116.3 1.1 copy.60
  (68 shorter events, 8.5 us)
Async XLA Ops:
  2.5 14.6 %collective-permute-start = (f32[8,100,1,128]{3,0,2,1:T(8,128)}, f32[8,100,1,128]{3,0,2,1:T(8,128)}, u32[]{:S(2)}, u32[]{:S(2)}) collective-permute-start(f32[8,100,1,128]{3,0,2,1:T(8,128)} %get-tuple-element.166), channel_id=1, source_target_pairs={{8,0},{16,8},{24,16},{9,1},{17,9},{25,17},{10,2},{18,10},{26,18},{... | collective-permute-start | bytes 1228808 | tf_op jit(solution)/shard_map/ppermute | solution.py:21
  3.8 4.9 %copy-start.7 = (f32[2,128]{1,0:T(2,128)S(1)}, f32[2,128]{1,0:T(2,128)}, u32[]{:S(2)}) copy-start(f32[2,128]{1,0:T(2,128)} %param.23) | copy-start | bytes 3076
  3.8 4.9 %copy-start.8 = (f32[2,128]{1,0:T(2,128)S(1)}, f32[2,128]{1,0:T(2,128)}, u32[]{:S(2)}) copy-start(f32[2,128]{1,0:T(2,128)} %param.24) | copy-start | bytes 3076
  4.2 5.9 %collective-permute-start.1 = (f32[8,100,2,1]{1,0,3,2:T(8,128)S(1)}, f32[8,100,2,1]{1,0,3,2:T(8,128)S(1)}, u32[]{:S(2)}, u32[]{:S(2)}) collective-permute-start(f32[8,100,2,1]{1,0,3,2:T(8,128)S(1)} %copy.34), channel_id=1, source_target_pairs={{1,0},{2,1},{3,2},{4,3},{5,4},{6,5},{7,6},{0,7},{9,8},{10,9},{11,1... | collective-permute-start | bytes 19208 | tf_op jit(solution)/shard_map/ppermute | solution.py:15
  8.7 8.4 %copy-start.9 = (f32[2,128]{1,0:T(2,128)}, f32[2,128]{1,0:T(2,128)S(1)}, u32[]{:S(2)}) copy-start(f32[2,128]{1,0:T(2,128)S(1)} %subtract_subtract_fusion) | copy-start | bytes 3076
  9.0 8.1 %copy-start.2 = (bf16[8,100,2,128]{3,2,1,0:T(2,128)(2,1)S(1)}, bf16[8,100,2,128]{3,2,1,0:T(2,128)(2,1)}, u32[]{:S(2)}) copy-start(bf16[8,100,2,128]{3,2,1,0:T(2,128)(2,1)} %param.20) | copy-start | bytes 1228804
  18.5 2.4 %copy-start.4 = (bf16[3,8,100,100]{3,1,2,0:T(8,128)(2,1)S(1)}, bf16[3,8,100,100]{3,1,2,0:T(8,128)(2,1)}, u32[]{:S(2)}) copy-start(bf16[3,8,100,100]{3,1,2,0:T(8,128)(2,1)} %param.22) | copy-start | bytes 1440004
  19.4 1.5 %copy-start.3 = (bf16[2,8,100,2,128]{4,3,2,1,0:T(2,128)(2,1)S(1)}, bf16[2,8,100,2,128]{4,3,2,1,0:T(2,128)(2,1)}, u32[]{:S(2)}) copy-start(bf16[2,8,100,2,128]{4,3,2,1,0:T(2,128)(2,1)} %param.21) | copy-start | bytes 2457604
  19.4 13.6 %collective-permute-start.2 = (f32[8,100,1,128]{3,0,2,1:T(8,128)}, f32[8,100,1,128]{3,0,2,1:T(8,128)}, u32[]{:S(2)}, u32[]{:S(2)}) collective-permute-start(f32[8,100,1,128]{3,0,2,1:T(8,128)} %get-tuple-element.164), channel_id=1, source_target_pairs={{8,0},{16,8},{24,16},{9,1},{17,9},{25,17},{10,2},{18,10},{26,18},{... | collective-permute-start | bytes 1228808 | tf_op jit(solution)/shard_map/ppermute | solution.py:21
  22.3 2.8 %copy-start.6 = (s32[8,2,128]{2,1,0:T(2,128)S(1)}, s32[8,2,128]{2,1,0:T(2,128)}, u32[]{:S(2)}) copy-start(s32[8,2,128]{2,1,0:T(2,128)} %param.27) | copy-start | bytes 24580
  22.6 6.2 %collective-permute-start.3 = (f32[8,100,2,1]{1,0,3,2:T(8,128)S(1)}, f32[8,100,2,1]{1,0,3,2:T(8,128)}, u32[]{:S(2)}, u32[]{:S(2)}) collective-permute-start(f32[8,100,2,1]{1,0,3,2:T(8,128)S(1)} %copy.36), channel_id=1, source_target_pairs={{1,0},{2,1},{3,2},{4,3},{5,4},{6,5},{7,6},{0,7},{9,8},{10,9},{11,1... | collective-permute-start | bytes 19208 | tf_op jit(solution)/shard_map/ppermute | solution.py:15
  30.0 3.0 %copy-start.10 = (f32[2,128]{1,0:T(2,128)S(1)}, f32[2,128]{1,0:T(2,128)}, u32[]{:S(2)}) copy-start(f32[2,128]{1,0:T(2,128)} %copy-done.9) | copy-start | bytes 3076
  39.5 12.6 %copy-start.1 = (f32[8,100,1,128]{3,0,2,1:T(8,128)}, f32[8,100,1,128]{3,0,2,1:T(8,128)S(1)}, u32[]{:S(2)}) copy-start(f32[8,100,1,128]{3,0,2,1:T(8,128)S(1)} %get-tuple-element.161) | copy-start | bytes 1228804
  39.5 12.6 %collective-permute-start.4 = (f32[8,100,1,128]{3,0,2,1:T(8,128)}, f32[8,100,1,128]{3,0,2,1:T(8,128)}, u32[]{:S(2)}, u32[]{:S(2)}) collective-permute-start(f32[8,100,1,128]{3,0,2,1:T(8,128)} %get-tuple-element.162), channel_id=1, source_target_pairs={{8,0},{16,8},{24,16},{9,1},{17,9},{25,17},{10,2},{18,10},{26,18},{... | collective-permute-start | bytes 1228808 | tf_op jit(solution)/shard_map/ppermute | solution.py:21
  41.8 2.1 %collective-permute-start.5 = (f32[8,100,2,1]{1,0,3,2:T(8,128)}, f32[8,100,2,1]{1,0,3,2:T(8,128)}, u32[]{:S(2)}, u32[]{:S(2)}) collective-permute-start(f32[8,100,2,1]{1,0,3,2:T(8,128)} %copy.49), channel_id=1, source_target_pairs={{1,0},{2,1},{3,2},{4,3},{5,4},{6,5},{7,6},{0,7},{9,8},{10,9},{11,1... | collective-permute-start | bytes 19208 | tf_op jit(solution)/shard_map/ppermute | solution.py:15
  45.9 6.2 %copy-start.11 = (f32[2,128]{1,0:T(2,128)S(1)}, f32[2,128]{1,0:T(2,128)}, u32[]{:S(2)}) copy-start(f32[2,128]{1,0:T(2,128)} %copy-done.9) | copy-start | bytes 3076
  54.8 11.7 %collective-permute-start.6 = (f32[8,100,1,128]{3,0,2,1:T(8,128)}, f32[8,100,1,128]{3,0,2,1:T(8,128)}, u32[]{:S(2)}, u32[]{:S(2)}) collective-permute-start(f32[8,100,1,128]{3,0,2,1:T(8,128)} %get-tuple-element.160), channel_id=1, source_target_pairs={{8,0},{16,8},{24,16},{9,1},{17,9},{25,17},{10,2},{18,10},{26,18},{... | collective-permute-start | bytes 1228808 | tf_op jit(solution)/shard_map/ppermute | solution.py:21
  57.0 3.0 %collective-permute-start.7 = (f32[8,100,2,1]{1,0,3,2:T(8,128)}, f32[8,100,2,1]{1,0,3,2:T(8,128)}, u32[]{:S(2)}, u32[]{:S(2)}) collective-permute-start(f32[8,100,2,1]{1,0,3,2:T(8,128)} %copy.51), channel_id=1, source_target_pairs={{1,0},{2,1},{3,2},{4,3},{5,4},{6,5},{7,6},{0,7},{9,8},{10,9},{11,1... | collective-permute-start | bytes 19208 | tf_op jit(solution)/shard_map/ppermute | solution.py:15
  60.1 6.4 %copy-start = (f32[8,100,2,1]{3,0,2,1:T(8,128)S(1)}, f32[8,100,2,1]{3,0,2,1:T(8,128)}, u32[]{:S(2)}) copy-start(f32[8,100,2,1]{3,0,2,1:T(8,128)} %copy.50) | copy-start | bytes 19204
  66.5 0.7 copy-start.12
  74.1 0.9 copy-start.5
  75.2 0.7 copy-start.13
where the time goes:
time: 119 us; the launch traced here: 118 us
  blocking collectives  40.3 us (34%)
  waiting for transfers between devices  22.6 us (19%)
  local copies, waits for them, and re-layouts  21.5 us (18%)
  starting transfers between devices  13.5 us (11%)
  other arithmetic  8.79 us (7%)
  matrix products  7.96 us (7%)
  between operations  2.85 us (2%)
    psum x1, blocking collectives, per_device(): total = lax.psum(partial_value, ('lat', 'lon'))  40.3 us
    ppermute x4, waiting for transfers between devices, from_behind(): return lax.ppermute(block, axis, route)  20.2 us
    ppermute x4, starting transfers between devices, shifted(): return lax.ppermute(block, axis, route)  8.28 us
    dot_general x18, matrix products, transposed(): lax.dot_general(mats, right_side, (((1,), (1,)), ((0,), (0,))), preferred...  7.79 us
    ppermute x4, local copies, waits for them, and re-layouts, shifted(): return lax.ppermute(block, axis, route)  5.64 us
    add x3, other arithmetic, advect(): return (1.0 - clon - clat) * lam + clat * down + clon * right  5.49 us
    ppermute x4, starting transfers between devices, from_behind(): return lax.ppermute(block, axis, route)  5.25 us
    unnamed x36, local copies, waits for them, and re-layouts  5.18 us
  transfers between devices with their start and end apart: 8, of which 6 were waited for; matrix products, arithmetic and copies ran while one was open for 12% of the time, Pallas kernels for 0%

commit v1 on v0

--- a/solution.py
+++ b/solution.py
@@ -81,7 +81,9 @@
         precision=lax.Precision.HIGHEST,
         preferred_element_type=jnp.float32,
     )
-    total = lax.psum(partial_value, ("lat", "lon"))
+    total = partial_value
+    for q in ("lon", "lat"):
+        total = lax.psum(total, q)
     share = REG_DEV
     grad = lax.dynamic_slice_in_dim(total, lax.axis_index(("lat", "lon")) * share, share, 0)
     return (lam.astype(jnp.bfloat16), grad)

time: 119 us -> 122 us (1.025)
  blocking collectives: 40.3 us -> 43.2 us
    psum x1 -> x2, blocking collectives: 40.3 us -> 43.2 us  [per_device(): total = lax.psum(total, q)]
where the time goes in v1:
time: 122 us; the launch traced here: 121 us
  blocking collectives  43.2 us (35%)
  waiting for transfers between devices  22.4 us (18%)
  local copies, waits for them, and re-layouts  21.6 us (18%)
  starting transfers between devices  13.5 us (11%)
  other arithmetic  8.82 us (7%)
  matrix products  7.96 us (7%)
  between operations  2.95 us (2%)
    psum x2, blocking collectives, per_device(): total = lax.psum(total, q)  43.2 us
    ppermute x4, waiting for transfers between devices, from_behind(): return lax.ppermute(block, axis, route)  20.1 us
    ppermute x4, starting transfers between devices, shifted(): return lax.ppermute(block, axis, route)  8.27 us
    dot_general x18, matrix products, transposed(): lax.dot_general(mats, right_side, (((1,), (1,)), ((0,), (0,))), preferred...  7.79 us
    ppermute x4, local copies, waits for them, and re-layouts, shifted(): return lax.ppermute(block, axis, route)  5.66 us
    add x3, other arithmetic, advect(): return (1.0 - clon - clat) * lam + clat * down + clon * right  5.49 us
    ppermute x4, starting transfers between devices, from_behind(): return lax.ppermute(block, axis, route)  5.25 us
    unnamed x36, local copies, waits for them, and re-layouts  5.21 us
  transfers between devices with their start and end apart: 8, of which 6 were waited for; matrix products, arithmetic and copies ran while one was open for 12% of the time, Pallas kernels for 0%

profile of v1, /device:TPU:0, one launch (start us, length us, event | category | flops | bytes accessed | tf_op | source)
XLA Modules:
  0.0 120.8 jit_solution(7805891861508252120)
XLA Ops:
  0.6 1.1 copy_convert_fusion.5
  1.7 0.8 fusion.83
  2.5 1.3 %collective-permute-start = (f32[8,100,1,128]{3,0,2,1:T(8,128)}, f32[8,100,1,128]{3,0,2,1:T(8,128)}, u32[]{:S(2)}, u32[]{:S(2)}) collective-permute-start(f32[8,100,1,128]{3,0,2,1:T(8,128)} %get-tuple-element.166), channel_id=1, source_target_pairs={{8,0},{16,8},{24,16},{9,1},{17,9},{25,17},{10,2},{18,10},{26,18},{... | collective-permute-start | bytes 1228808 | tf_op jit(solution)/shard_map/ppermute | solution.py:21
  4.2 4.5 %collective-permute-start.1 = (f32[8,100,2,1]{1,0,3,2:T(8,128)S(1)}, f32[8,100,2,1]{1,0,3,2:T(8,128)S(1)}, u32[]{:S(2)}, u32[]{:S(2)}) collective-permute-start(f32[8,100,2,1]{1,0,3,2:T(8,128)S(1)} %copy.34), channel_id=1, source_target_pairs={{1,0},{2,1},{3,2},{4,3},{5,4},{6,5},{7,6},{0,7},{9,8},{10,9},{11,1... | collective-permute-start | bytes 19208 | tf_op jit(solution)/shard_map/ppermute | solution.py:15
  9.0 1.1 collective-permute-done.1
  10.5 6.6 %collective-permute-done = f32[8,100,1,128]{3,0,2,1:T(8,128)} collective-permute-done((f32[8,100,1,128]{3,0,2,1:T(8,128)}, f32[8,100,1,128]{3,0,2,1:T(8,128)}, u32[]{:S(2)}, u32[]{:S(2)}) %collective-permute-start) | collective-permute-done | bytes 409632 | tf_op jit(solution)/shard_map/ppermute | solution.py:21
  17.1 1.3 %fusion.65 = f32[8,100,2,128]{3,0,2,1:T(8,128)S(1)} fusion(f32[8,100,1,128]{3,0,2,1:T(8,128)} %collective-permute-done, f32[8,100,1,128]{3,0,2,1:T(8,128)S(1)} %get-tuple-element.165, f32[8,100,2,1]{3,0,2,1:T(8,128)S(1)} %copy.35, f32[8,100,2,127]{3,0,2,1:T(8,128)S(1)} %slice.99, f32[2,128]{1,0:T(2,128)S(1)} %copy-done.7, f32[2,128]{1,0:T(2,128)S(1)} %copy-done.8, ...), kind=kLoop, calls=%fused_computation.86 | loop fusion | flops 1638400 | bytes 2870272 | tf_op jit(solution)/shard_map/add | solution.py:27
  18.5 1.0 fusion.82
  19.4 1.4 %collective-permute-start.2 = (f32[8,100,1,128]{3,0,2,1:T(8,128)}, f32[8,100,1,128]{3,0,2,1:T(8,128)}, u32[]{:S(2)}, u32[]{:S(2)}) collective-permute-start(f32[8,100,1,128]{3,0,2,1:T(8,128)} %get-tuple-element.164), channel_id=1, source_target_pairs={{8,0},{16,8},{24,16},{9,1},{17,9},{25,17},{10,2},{18,10},{26,18},{... | collective-permute-start | bytes 1228808 | tf_op jit(solution)/shard_map/ppermute | solution.py:21
  20.9 1.3 %fusion.79 = (bf16[1,8,100,2,128]{4,3,2,1,0:T(2,128)(2,1)}, bf16[1,8,100,2,128]{4,3,2,1,0:T(2,128)(2,1)S(1)}) fusion(bf16[2,8,100,2,128]{4,3,2,1,0:T(2,128)(2,1)S(1)} %copy-done.3), kind=kLoop, calls=%fused_computation.122 | loop fusion | bytes 1638400 | tf_op jit(solution)/shard_map/slice | solution.py:70
  22.6 2.4 %collective-permute-start.3 = (f32[8,100,2,1]{1,0,3,2:T(8,128)S(1)}, f32[8,100,2,1]{1,0,3,2:T(8,128)}, u32[]{:S(2)}, u32[]{:S(2)}) collective-permute-start(f32[8,100,2,1]{1,0,3,2:T(8,128)S(1)} %copy.36), channel_id=1, source_target_pairs={{1,0},{2,1},{3,2},{4,3},{5,4},{6,5},{7,6},{0,7},{9,8},{10,9},{11,1... | collective-permute-start | bytes 19208 | tf_op jit(solution)/shard_map/ppermute | solution.py:15
  25.1 0.7 compare_reduce_fusion
  28.9 1.1 copy.37
  30.1 2.9 %collective-permute-done.2 = f32[8,100,1,128]{3,0,2,1:T(8,128)} collective-permute-done((f32[8,100,1,128]{3,0,2,1:T(8,128)}, f32[8,100,1,128]{3,0,2,1:T(8,128)}, u32[]{:S(2)}, u32[]{:S(2)}) %collective-permute-start.2) | collective-permute-done | bytes 409632 | tf_op jit(solution)/shard_map/ppermute | solution.py:21
  33.0 1.4 %fusion.68 = f32[8,100,256]{2,0,1:T(8,128)S(1)} fusion(f32[8,100,1,128]{3,0,2,1:T(8,128)} %collective-permute-done.2, f32[8,100,1,128]{3,0,2,1:T(8,128)} %get-tuple-element.163, f32[8,100,2,1]{3,0,2,1:T(8,128)S(1)} %copy.37, f32[8,100,2,127]{3,0,2,1:T(8,128)S(1)} %slice.103, f32[8,100,2,128]{3,0,2,1:T(8,128)S(1)} %fusion.65, f32[2,128]{1,0:T(2,128)S(1)} %copy-done.7, ...), kind=kLoop, calls=%fused_computation.91 | loop fusion | flops 1433600 | bytes 3279872 | tf_op jit(solution)/shard_map/reshape | solution.py:46
  34.4 1.3 %conditional.6 = (f32[8,100,256]{2,1,0:T(8,128)S(1)}) conditional(s32[]{:T(128)} %convert_element_type.102, (f32[8,100,256]{2,0,1:T(8,128)S(1)}) %tuple.65, (s32[8,1,256]{2,0,1:T(8,128)S(1)}, f32[8,100,256]{2,0,1:T(8,128)S(1)}, bf16[8,100,100]{1,2,0:T(8,128)(2,1)S(1)}, bf16[8,100,256]{2,0,1:T(8,128)(2,1)S(1)}) %tuple.94), branch_computations={%region_3.4_spmd, %region_4.5_spmd} | conditional | flops 125749248 | bytes 7865096 | solution.py:59
  35.8 1.3 %conditional.7 = (f32[8,100,256]{2,1,0:T(8,128)S(1)}) conditional(s32[]{:T(128)} %convert_element_type.101, f32[8,100,256]{2,1,0:T(8,128)S(1)} %get-tuple-element.170, (s32[8,1,256]{2,0,1:T(8,128)S(1)}, f32[8,100,256]{2,1,0:T(8,128)S(1)}, bf16[8,100,100]{1,2,0:T(8,128)(2,1)S(1)}, bf16[8,100,256]{2,0,1:T(8,128)(2,1)S(1)}) %tuple.98), branch_computations={%region_5.6_spmd, %region_6.7_spmd} | conditional | flops 125954048 | bytes 7865096 | solution.py:59
  36.4 0.8 fusion.12
  37.1 1.3 %conditional.8 = (f32[8,100,256]{2,1,0:T(8,128)S(1)}) conditional(s32[]{:T(128)} %convert_element_type.100, f32[8,100,256]{2,1,0:T(8,128)S(1)} %get-tuple-element.171, (s32[8,1,256]{2,0,1:T(8,128)S(1)}, f32[8,100,256]{2,1,0:T(8,128)S(1)}, bf16[8,100,100]{1,2,0:T(8,128)(2,1)S(1)}, bf16[8,100,256]{2,0,1:T(8,128)(2,1)S(1)}) %tuple.96), branch_computations={%region_7.8_spmd, %region_8.9_spmd} | conditional | flops 125954048 | bytes 7865096 | solution.py:59
  37.7 0.8 fusion.23
  38.7 0.8 fusion.81
  39.6 1.3 %collective-permute-start.4 = (f32[8,100,1,128]{3,0,2,1:T(8,128)}, f32[8,100,1,128]{3,0,2,1:T(8,128)}, u32[]{:S(2)}, u32[]{:S(2)}) collective-permute-start(f32[8,100,1,128]{3,0,2,1:T(8,128)} %get-tuple-element.162), channel_id=1, source_target_pairs={{8,0},{16,8},{24,16},{9,1},{17,9},{25,17},{10,2},{18,10},{26,18},{... | collective-permute-start | bytes 1228808 | tf_op jit(solution)/shard_map/ppermute | solution.py:21
  40.8 1.0 copy.49
  42.6 1.3 %collective-permute-done.5 = f32[8,100,2,1]{1,0,3,2:T(8,128)} collective-permute-done((f32[8,100,2,1]{1,0,3,2:T(8,128)}, f32[8,100,2,1]{1,0,3,2:T(8,128)}, u32[]{:S(2)}, u32[]{:S(2)}) %collective-permute-start.5) | collective-permute-done | bytes 6432 | tf_op jit(solution)/shard_map/ppermute | solution.py:15
  43.9 2.0 %copy.50 = f32[8,100,2,1]{3,0,2,1:T(8,128)} copy(f32[8,100,2,1]{1,0,3,2:T(8,128)} %collective-permute-done.5) | data formatting | bytes 12800 | tf_op jit(solution)/shard_map/ppermute | solution.py:15
  45.9 6.2 %collective-permute-done.4 = f32[8,100,1,128]{3,0,2,1:T(8,128)} collective-permute-done((f32[8,100,1,128]{3,0,2,1:T(8,128)}, f32[8,100,1,128]{3,0,2,1:T(8,128)}, u32[]{:S(2)}, u32[]{:S(2)}) %collective-permute-start.4) | collective-permute-done | bytes 409632 | tf_op jit(solution)/shard_map/ppermute | solution.py:21
  52.2 1.7 %multiply_add_fusion = f32[8,100,2,128]{3,0,2,1:T(8,128)S(1)} fusion(f32[8,100,1,128]{3,0,2,1:T(8,128)} %collective-permute-done.4, f32[8,100,1,128]{3,0,2,1:T(8,128)S(1)} %get-tuple-element.161, f32[2,128]{1,0:T(2,128)S(1)} %copy-done.7, f32[2,128]{1,0:T(2,128)S(1)} %copy-done.8, f32[2,128]{1,0:T(2,128)S(1)} %copy-done.11, f32[8,100,2,1]{3,0,2,1:T(8,128)} %copy.50, ...), kind=kLoop, calls=%fused_computation.107 | loop fusion | flops 1433600 | bytes 3279872 | tf_op jit(solution)/shard_map/add | solution.py:27
  53.8 1.0 fusion.80
  54.8 1.3 %collective-permute-start.6 = (f32[8,100,1,128]{3,0,2,1:T(8,128)}, f32[8,100,1,128]{3,0,2,1:T(8,128)}, u32[]{:S(2)}, u32[]{:S(2)}) collective-permute-start(f32[8,100,1,128]{3,0,2,1:T(8,128)} %get-tuple-element.160), channel_id=1, source_target_pairs={{8,0},{16,8},{24,16},{9,1},{17,9},{25,17},{10,2},{18,10},{26,18},{... | collective-permute-start | bytes 1228808 | tf_op jit(solution)/shard_map/ppermute | solution.py:21
  56.1 1.0 copy.51
  57.0 0.8 collective-permute-start.7
  57.8 1.1 copy.137
  58.9 1.2 %slice.111 = f32[8,100,2,127]{3,0,2,1:T(8,128)} slice(f32[8,100,2,128]{3,0,2,1:T(8,128)S(1)} %multiply_add_fusion), slice={[0:8], [0:100], [0:2], [1:128]} | slice | bytes 1625600 | tf_op jit(solution)/shard_map/slice | solution.py:25
  60.1 2.1 %copy.52 = f32[8,100,2,1]{3,0,2,1:T(8,128)} copy(f32[8,100,2,1]{1,0,3,2:T(8,128)} %collective-permute-done.7) | data formatting | bytes 12800 | tf_op jit(solution)/shard_map/ppermute | solution.py:15
  62.2 4.3 %collective-permute-done.6 = f32[8,100,1,128]{3,0,2,1:T(8,128)} collective-permute-done((f32[8,100,1,128]{3,0,2,1:T(8,128)}, f32[8,100,1,128]{3,0,2,1:T(8,128)}, u32[]{:S(2)}, u32[]{:S(2)}) %collective-permute-start.6) | collective-permute-done | bytes 409632 | tf_op jit(solution)/shard_map/ppermute | solution.py:21
  66.5 0.7 copy-done.12
  67.2 2.5 %fusion.71 = f32[8,100,256]{2,0,1:T(8,128)S(1)} fusion(f32[8,100,1,128]{3,0,2,1:T(8,128)} %collective-permute-done.6, f32[8,100,1,128]{3,0,2,1:T(8,128)} %get-tuple-element.159, f32[8,100,2,1]{3,0,2,1:T(8,128)} %copy.52, f32[8,100,2,127]{3,0,2,1:T(8,128)} %slice.111, f32[8,100,256]{2,1,0:T(8,128)S(1)} %get-tuple-element.172, ...), kind=kLoop, calls=%fused_computation.98 | loop fusion | flops 2867200 | bytes 4918272 | tf_op jit(solution)/shard_map/add | solution.py:27
  69.7 1.5 %conditional.9 = (f32[8,100,256]{2,1,0:T(8,128)S(1)}) conditional(s32[]{:T(128)} %convert_element_type.102, (f32[8,100,256]{2,0,1:T(8,128)S(1)}) %tuple.66, (s32[8,1,256]{2,0,1:T(8,128)S(1)}, f32[8,100,256]{2,0,1:T(8,128)S(1)}, bf16[8,100,100]{1,2,0:T(8,128)(2,1)S(1)}, bf16[8,100,256]{2,0,1:T(8,128)(2,1)S(1)}) %tuple.95), branch_computations={%region_9.10_spmd, %region_10.11_spmd} | conditional | flops 125749248 | bytes 7865096 | solution.py:59
  70.6 0.6 fusion.34
  71.2 1.3 %conditional.10 = (f32[8,100,256]{2,1,0:T(8,128)S(1)}) conditional(s32[]{:T(128)} %convert_element_type.101, f32[8,100,256]{2,1,0:T(8,128)S(1)} %get-tuple-element.173, (s32[8,1,256]{2,0,1:T(8,128)S(1)}, f32[8,100,256]{2,1,0:T(8,128)S(1)}, bf16[8,100,100]{1,2,0:T(8,128)(2,1)S(1)}, bf16[8,100,256]{2,0,1:T(8,128)(2,1)S(1)}) %tuple.99), branch_computations={%region_11.12_spmd, %region_12.13_spmd} | conditional | flops 125954048 | bytes 7865096 | solution.py:59
  71.8 0.8 fusion.44
  72.6 1.3 %conditional.11 = (f32[8,100,256]{2,1,0:T(8,128)S(1)}) conditional(s32[]{:T(128)} %convert_element_type.100, f32[8,100,256]{2,1,0:T(8,128)S(1)} %get-tuple-element.174, (s32[8,1,256]{2,0,1:T(8,128)S(1)}, f32[8,100,256]{2,1,0:T(8,128)S(1)}, bf16[8,100,100]{1,2,0:T(8,128)(2,1)S(1)}, bf16[8,100,256]{2,0,1:T(8,128)(2,1)S(1)}) %tuple.97), branch_computations={%region_13.14_spmd, %region_14.15_spmd} | conditional | flops 125954048 | bytes 7865096 | solution.py:59
  73.2 0.8 fusion.55
  74.3 0.8 copy-done.5
  75.2 0.7 copy-done.13
  76.1 26.0 %psum.14 = f32[32,100]{1,0:T(8,128)S(1)} all-reduce(f32[32,100]{1,0:T(8,128)S(1)} %fusion.77), channel_id=1, replica_groups=mesh['lat'=4,'lon'=8] {'lon'}, use_global_device_ids=true, to_apply=%region_15.16 | all-reduce | flops 3200 | bytes 25600 | tf_op jit(solution)/shard_map/psum | solution.py:86
  102.1 17.2 %psum.15 = f32[32,100]{1,0:T(8,128)S(1)} all-reduce(f32[32,100]{1,0:T(8,128)S(1)} %psum.14), channel_id=1, replica_groups=mesh['lat'=4,'lon'=8] {'lat'}, use_global_device_ids=true, to_apply=%region_16.17 | all-reduce | flops 3200 | bytes 25600 | tf_op jit(solution)/shard_map/psum | solution.py:86
  119.3 1.1 copy.60
  (69 shorter events, 9.1 us)
Async XLA Ops:
  2.5 14.6 %collective-permute-start = (f32[8,100,1,128]{3,0,2,1:T(8,128)}, f32[8,100,1,128]{3,0,2,1:T(8,128)}, u32[]{:S(2)}, u32[]{:S(2)}) collective-permute-start(f32[8,100,1,128]{3,0,2,1:T(8,128)} %get-tuple-element.166), channel_id=1, source_target_pairs={{8,0},{16,8},{24,16},{9,1},{17,9},{25,17},{10,2},{18,10},{26,18},{... | collective-permute-start | bytes 1228808 | tf_op jit(solution)/shard_map/ppermute | solution.py:21
  3.8 4.9 %copy-start.7 = (f32[2,128]{1,0:T(2,128)S(1)}, f32[2,128]{1,0:T(2,128)}, u32[]{:S(2)}) copy-start(f32[2,128]{1,0:T(2,128)} %param.23) | copy-start | bytes 3076
  3.8 4.9 %copy-start.8 = (f32[2,128]{1,0:T(2,128)S(1)}, f32[2,128]{1,0:T(2,128)}, u32[]{:S(2)}) copy-start(f32[2,128]{1,0:T(2,128)} %param.24) | copy-start | bytes 3076
  4.2 5.9 %collective-permute-start.1 = (f32[8,100,2,1]{1,0,3,2:T(8,128)S(1)}, f32[8,100,2,1]{1,0,3,2:T(8,128)S(1)}, u32[]{:S(2)}, u32[]{:S(2)}) collective-permute-start(f32[8,100,2,1]{1,0,3,2:T(8,128)S(1)} %copy.34), channel_id=1, source_target_pairs={{1,0},{2,1},{3,2},{4,3},{5,4},{6,5},{7,6},{0,7},{9,8},{10,9},{11,1... | collective-permute-start | bytes 19208 | tf_op jit(solution)/shard_map/ppermute | solution.py:15
  8.7 8.4 %copy-start.9 = (f32[2,128]{1,0:T(2,128)}, f32[2,128]{1,0:T(2,128)S(1)}, u32[]{:S(2)}) copy-start(f32[2,128]{1,0:T(2,128)S(1)} %subtract_subtract_fusion) | copy-start | bytes 3076
  9.0 8.1 %copy-start.2 = (bf16[8,100,2,128]{3,2,1,0:T(2,128)(2,1)S(1)}, bf16[8,100,2,128]{3,2,1,0:T(2,128)(2,1)}, u32[]{:S(2)}) copy-start(bf16[8,100,2,128]{3,2,1,0:T(2,128)(2,1)} %param.20) | copy-start | bytes 1228804
  18.5 2.4 %copy-start.4 = (bf16[3,8,100,100]{3,1,2,0:T(8,128)(2,1)S(1)}, bf16[3,8,100,100]{3,1,2,0:T(8,128)(2,1)}, u32[]{:S(2)}) copy-start(bf16[3,8,100,100]{3,1,2,0:T(8,128)(2,1)} %param.22) | copy-start | bytes 1440004
  19.4 1.5 %copy-start.3 = (bf16[2,8,100,2,128]{4,3,2,1,0:T(2,128)(2,1)S(1)}, bf16[2,8,100,2,128]{4,3,2,1,0:T(2,128)(2,1)}, u32[]{:S(2)}) copy-start(bf16[2,8,100,2,128]{4,3,2,1,0:T(2,128)(2,1)} %param.21) | copy-start | bytes 2457604
  19.4 13.6 %collective-permute-start.2 = (f32[8,100,1,128]{3,0,2,1:T(8,128)}, f32[8,100,1,128]{3,0,2,1:T(8,128)}, u32[]{:S(2)}, u32[]{:S(2)}) collective-permute-start(f32[8,100,1,128]{3,0,2,1:T(8,128)} %get-tuple-element.164), channel_id=1, source_target_pairs={{8,0},{16,8},{24,16},{9,1},{17,9},{25,17},{10,2},{18,10},{26,18},{... | collective-permute-start | bytes 1228808 | tf_op jit(solution)/shard_map/ppermute | solution.py:21
  22.2 2.8 %copy-start.6 = (s32[8,2,128]{2,1,0:T(2,128)S(1)}, s32[8,2,128]{2,1,0:T(2,128)}, u32[]{:S(2)}) copy-start(s32[8,2,128]{2,1,0:T(2,128)} %param.27) | copy-start | bytes 24580
  22.6 6.3 %collective-permute-start.3 = (f32[8,100,2,1]{1,0,3,2:T(8,128)S(1)}, f32[8,100,2,1]{1,0,3,2:T(8,128)}, u32[]{:S(2)}, u32[]{:S(2)}) collective-permute-start(f32[8,100,2,1]{1,0,3,2:T(8,128)S(1)} %copy.36), channel_id=1, source_target_pairs={{1,0},{2,1},{3,2},{4,3},{5,4},{6,5},{7,6},{0,7},{9,8},{10,9},{11,1... | collective-permute-start | bytes 19208 | tf_op jit(solution)/shard_map/ppermute | solution.py:15
  30.1 2.9 %copy-start.10 = (f32[2,128]{1,0:T(2,128)S(1)}, f32[2,128]{1,0:T(2,128)}, u32[]{:S(2)}) copy-start(f32[2,128]{1,0:T(2,128)} %copy-done.9) | copy-start | bytes 3076
  39.6 12.6 %copy-start.1 = (f32[8,100,1,128]{3,0,2,1:T(8,128)}, f32[8,100,1,128]{3,0,2,1:T(8,128)S(1)}, u32[]{:S(2)}) copy-start(f32[8,100,1,128]{3,0,2,1:T(8,128)S(1)} %get-tuple-element.161) | copy-start | bytes 1228804
  39.6 12.6 %collective-permute-start.4 = (f32[8,100,1,128]{3,0,2,1:T(8,128)}, f32[8,100,1,128]{3,0,2,1:T(8,128)}, u32[]{:S(2)}, u32[]{:S(2)}) collective-permute-start(f32[8,100,1,128]{3,0,2,1:T(8,128)} %get-tuple-element.162), channel_id=1, source_target_pairs={{8,0},{16,8},{24,16},{9,1},{17,9},{25,17},{10,2},{18,10},{26,18},{... | collective-permute-start | bytes 1228808 | tf_op jit(solution)/shard_map/ppermute | solution.py:21
  41.8 2.1 %collective-permute-start.5 = (f32[8,100,2,1]{1,0,3,2:T(8,128)}, f32[8,100,2,1]{1,0,3,2:T(8,128)}, u32[]{:S(2)}, u32[]{:S(2)}) collective-permute-start(f32[8,100,2,1]{1,0,3,2:T(8,128)} %copy.49), channel_id=1, source_target_pairs={{1,0},{2,1},{3,2},{4,3},{5,4},{6,5},{7,6},{0,7},{9,8},{10,9},{11,1... | collective-permute-start | bytes 19208 | tf_op jit(solution)/shard_map/ppermute | solution.py:15
  45.9 6.2 %copy-start.11 = (f32[2,128]{1,0:T(2,128)S(1)}, f32[2,128]{1,0:T(2,128)}, u32[]{:S(2)}) copy-start(f32[2,128]{1,0:T(2,128)} %copy-done.9) | copy-start | bytes 3076
  54.8 11.7 %collective-permute-start.6 = (f32[8,100,1,128]{3,0,2,1:T(8,128)}, f32[8,100,1,128]{3,0,2,1:T(8,128)}, u32[]{:S(2)}, u32[]{:S(2)}) collective-permute-start(f32[8,100,1,128]{3,0,2,1:T(8,128)} %get-tuple-element.160), channel_id=1, source_target_pairs={{8,0},{16,8},{24,16},{9,1},{17,9},{25,17},{10,2},{18,10},{26,18},{... | collective-permute-start | bytes 1228808 | tf_op jit(solution)/shard_map/ppermute | solution.py:21
  57.0 3.1 %collective-permute-start.7 = (f32[8,100,2,1]{1,0,3,2:T(8,128)}, f32[8,100,2,1]{1,0,3,2:T(8,128)}, u32[]{:S(2)}, u32[]{:S(2)}) collective-permute-start(f32[8,100,2,1]{1,0,3,2:T(8,128)} %copy.51), channel_id=1, source_target_pairs={{1,0},{2,1},{3,2},{4,3},{5,4},{6,5},{7,6},{0,7},{9,8},{10,9},{11,1... | collective-permute-start | bytes 19208 | tf_op jit(solution)/shard_map/ppermute | solution.py:15
  60.1 6.4 %copy-start = (f32[8,100,2,1]{3,0,2,1:T(8,128)S(1)}, f32[8,100,2,1]{3,0,2,1:T(8,128)}, u32[]{:S(2)}) copy-start(f32[8,100,2,1]{3,0,2,1:T(8,128)} %copy.50) | copy-start | bytes 19204
  66.5 0.7 copy-start.12
  74.2 0.9 copy-start.5
  75.2 0.7 copy-start.13
